TPU v7x, 128 devices: a whole 4x4x4 slice. The times are simulated.
128 devices in a mesh: ep: 32 (over z, x, core), dp: 4 (over y).
Axes of the slice: x: 4, y: 4, z: 4, core: 2. Of those that a mesh axis runs over, the one named last changes fastest.
Arguments:
- grad_out: float32 [16384, 1536], P(('ep', 'dp')), may hold values from -6 to 6
- tokens: bfloat16 [16384, 1536], P(('ep', 'dp')), may hold values from -6 to 6
- probs: float32 [16384, 4], P(('ep', 'dp')), may hold values from 0.1 to 0.5
- expert_ids: int32 [16384, 4], P(('ep', 'dp')), may hold values from 0 to 31, all different within a row; in each aligned block of 128 rows (0 to 127, 128 to 255, ...) at most 20 rows name the same one
- priority: int32 [128, 128], P(('ep', 'dp')), may hold values from 0 to 127, each once within a row
- cap_counts: int32 [32], replicated, may hold values from 10 to 20, as said below
- gate_weight: bfloat16 [32, 1536, 1536], P('ep'), may hold values from -0.15625 to 0.15625
- up_weight: bfloat16 [32, 1536, 1536], P('ep'), may hold values from -0.15625 to 0.15625
- down_weight: bfloat16 [32, 1536, 1536], P('ep'), may hold values from -0.15625 to 0.15625
Outputs:
- input_grad: bfloat16 [16384, 1536], P(('ep', 'dp'))
- prob_grad: float32 [16384, 4], P(('ep', 'dp'))
- gate_grad: bfloat16 [32, 1536, 1536], P('ep', 'dp')
- up_grad: bfloat16 [32, 1536, 1536], P('ep', 'dp')
- down_grad: bfloat16 [32, 1536, 1536], P('ep', 'dp')
Inputs may be any that keep to these rules, and one draw needn't show every extreme that they name: `expert_ids`: each row names 4 different experts; among the rows of one device no expert is named by more than 20 rows, and in some device some expert is named by exactly 20 rows. `priority`: each row orders the 128 tokens of one device, each number once. `cap_counts`: some expert has exactly 20.
All inputs are finite; a program needn't handle non-finite values. Where the computation divides by a largest or mean magnitude, that divisor is 1e-20 or more.
Results may differ from a plain program's by a relative error of at most 0.017.
Values may be sent and summed in bfloat16 or wider, within the bound.
A program may use at most 128 MiB of HBM per device.

v0:
```python
import jax
import jax.numpy as jnp
from jax import lax
from jax.sharding import PartitionSpec as P

sharpness = 1.702


def contract_last(first_op, second_op):
    return lax.dot_general(
        first_op, second_op, (((1,), (1,)), ((), ())), preferred_element_type=jnp.float32
    )


def contract_first(first_op, second_op):
    return lax.dot_general(
        first_op, second_op, (((0,), (0,)), ((), ())), preferred_element_type=jnp.float32
    )


def route_table(expert_ids, priority, cap_counts, buckets, capacity):
    ranking = priority[0]
    earlier = (ranking[None, :] < ranking[:, None]).astype(jnp.float32)
    expert_range = lax.broadcasted_iota(jnp.int32, (1, 1, buckets), 2)
    matches = (expert_ids[:, :, None] == expert_range).astype(jnp.float32)
    routed = jnp.sum(matches, axis=1)
    before = jnp.dot(earlier, routed)
    slot_rank = jnp.sum(matches * before[:, None, :], axis=2)
    keep_limit = jnp.sum(matches * cap_counts.astype(jnp.float32)[None, None, :], axis=2)
    slot_range = lax.broadcasted_iota(jnp.float32, (1, 1, capacity), 2)
    slot_hit = (
        (slot_rank[:, :, None] == slot_range) & (slot_rank < keep_limit)[:, :, None]
    ).astype(jnp.float32)
    placement = matches[:, :, :, None] * slot_hit[:, :, None, :]
    return placement.reshape(expert_ids.shape[0], expert_ids.shape[1], buckets * capacity)


def deltas(slot_x, slot_g, w_gate, w_up, w_down):
    gate_pre = contract_last(slot_x, w_gate)
    up_pre = contract_last(slot_x, w_up)
    act_delta = contract_last(slot_g, w_down)
    squash = jax.nn.sigmoid(sharpness * gate_pre)
    gated = gate_pre * squash
    activated = (up_pre + 1.0) * gated
    up_delta = (act_delta * gated).astype(jnp.bfloat16)
    gate_delta = (
        act_delta * (up_pre + 1.0) * (squash + sharpness * gate_pre * squash * (1.0 - squash))
    ).astype(jnp.bfloat16)
    return (activated, act_delta, gate_delta, up_delta)


def on_device(
    grad_out, tokens, probs, expert_ids, priority, cap_counts, gate_weight, up_weight, down_weight
):
    ep_size = lax.axis_size("ep")
    dp_size = lax.axis_size("dp")
    tok_rows, model_width = tokens.shape
    route_count = expert_ids.shape[1]
    capacity = 5 * route_count * tok_rows // (4 * ep_size)
    slot_rows = ep_size * capacity
    placement = route_table(expert_ids, priority, cap_counts, ep_size, capacity)
    slot_table = jnp.sum(placement, axis=1)
    table_low = slot_table.astype(jnp.bfloat16)
    row_scale = jnp.maximum(jnp.max(jnp.abs(grad_out), axis=1), 1.0)
    quantized = (grad_out / row_scale[:, None]).astype(jnp.bfloat16)
    send_prob = jnp.sum(placement * probs[:, :, None], axis=(0, 1))
    send_scale = jnp.sum(slot_table * row_scale[:, None], axis=0)
    send_x = jnp.einsum("ts,td->sd", table_low, tokens, preferred_element_type=jnp.float32).astype(
        jnp.bfloat16
    )
    send_g = (
        jnp.einsum("ts,td->sd", table_low, quantized, preferred_element_type=jnp.float32)
        * (send_prob * send_scale)[:, None]
    ).astype(jnp.bfloat16)
    bucket_shape = (ep_size, capacity, model_width)

    def exchange(a):
        return lax.all_to_all(a, "ep", split_axis=0, concat_axis=0, tiled=True)

    slot_x = exchange(send_x.reshape(bucket_shape)).reshape(slot_rows, model_width)
    all_x = lax.all_gather(slot_x, "dp", axis=0, tiled=True)
    slot_g = exchange(send_g.reshape(bucket_shape)).reshape(slot_rows, model_width)
    all_g = lax.all_gather(slot_g, "dp", axis=0, tiled=True)
    w_gate = gate_weight[0]
    w_up = up_weight[0]
    w_down = down_weight[0]
    activated, act_delta, gate_delta, up_delta = deltas(slot_x, slot_g, w_gate, w_up, w_down)
    slot_in = (
        jnp.dot(gate_delta, w_gate, preferred_element_type=jnp.float32)
        + jnp.dot(up_delta, w_up, preferred_element_type=jnp.float32)
    ).astype(jnp.bfloat16)
    slot_out = jnp.sum(activated * act_delta, axis=1)
    back_in = exchange(slot_in.reshape(bucket_shape))
    back_prob = exchange(slot_out.reshape(ep_size, capacity).astype(jnp.bfloat16))
    prob_grad = jnp.einsum("tks,s->tk", placement, back_prob.reshape(slot_rows)) / probs
    input_grad = jnp.einsum(
        "ts,sd->td",
        table_low,
        back_in.reshape(slot_rows, model_width),
        preferred_element_type=jnp.float32,
    ).astype(jnp.bfloat16)
    share = w_gate.shape[0] // dp_size
    first = lax.axis_index("dp") * share

    def mine(w):
        return lax.dynamic_slice_in_dim(w, first, share, 0)

    act_mine, _, gd_mine, ud_mine = deltas(all_x, all_g, mine(w_gate), mine(w_up), mine(w_down))
    gate_share = contract_first(gd_mine, all_x).astype(jnp.bfloat16)
    up_share = contract_first(ud_mine, all_x).astype(jnp.bfloat16)
    down_share = contract_first(act_mine.astype(jnp.bfloat16), all_g).astype(jnp.bfloat16)
    return (input_grad, prob_grad, gate_share[None], up_share[None], down_share[None])


def solution(mesh):
    return jax.shard_map(
        on_device,
        mesh=mesh,
        in_specs=(
            P(("ep", "dp"), None),
            P(("ep", "dp"), None),
            P(("ep", "dp"), None),
            P(("ep", "dp"), None),
            P(("ep", "dp"), None),
            P(),
            P("ep", None, None),
            P("ep", None, None),
            P("ep", None, None),
        ),
        out_specs=(
            P(("ep", "dp"), None),
            P(("ep", "dp"), None),
            P("ep", "dp", None),
            P("ep", "dp", None),
            P("ep", "dp", None),
        ),
        check_vma=False,
    )
```

profile of v0, /device:TPU:1, one launch (start us, length us, event | category | flops | bytes accessed | tf_op | source)
XLA Modules:
  0.0 248.0 jit_solution(7221112332950681031)
XLA Ops:
  7.2 0.0 copy-start
  7.2 0.0 all-gather.5.cloned.1.call-start
  7.2 0.7 convert_element_type.78
  7.9 0.7 fusion.39
  8.6 0.8 select_reduce_fusion
  9.4 0.9 fusion.40
  10.3 0.7 select_reduce_fusion.1
  11.1 1.3 abs_reduce_fusion
  12.4 1.0 fusion.24
  13.3 0.2 multiply_reduce_fusion.2
  13.5 0.1 copy.29
  13.6 0.0 copy-done
  13.6 1.9 convolution_convert_fusion
  15.6 2.5 reshape.94
  18.0 40.7 %all_to_all.24 = bf16[32,20,1536]{2,1,0:T(8,128)(2,1)} all-to-all(bf16[32,20,1536]{2,1,0:T(8,128)(2,1)S(1)} %reshape.94), channel_id=1, replica_groups=mesh['ep'=32,'dp'=4] {'ep'}, dimensions={0} | all-to-all | bytes 3932160 | tf_op jit(solution)/shard_map/all_to_all | solution.py:78
  58.7 4.1 %reshape.95 = bf16[640,1536]{1,0:T(8,128)(2,1)} reshape(bf16[32,20,1536]{2,1,0:T(8,128)(2,1)} %all_to_all.24) | data formatting | bytes 3932160 | tf_op jit(solution)/shard_map/reshape | solution.py:80
  62.8 0.0 all-gather.5.cloned.1.call-update
  62.8 0.0 all-gather.3.cloned.1.call-start
  62.9 0.1 copy.30
  62.9 0.1 mul.136
  63.0 0.0 copy-done.4
  63.1 2.1 multiply_convert_fusion.5
  65.2 2.5 reshape.92
  67.6 35.0 %all_to_all.25 = bf16[32,20,1536]{2,1,0:T(8,128)(2,1)} all-to-all(bf16[32,20,1536]{2,1,0:T(8,128)(2,1)S(1)} %reshape.92), channel_id=1, replica_groups=mesh['ep'=32,'dp'=4] {'ep'}, dimensions={0} | all-to-all | bytes 3932160 | tf_op jit(solution)/shard_map/all_to_all | solution.py:78
  102.6 4.1 %reshape.93 = bf16[640,1536]{1,0:T(8,128)(2,1)} reshape(bf16[32,20,1536]{2,1,0:T(8,128)(2,1)} %all_to_all.25) | data formatting | bytes 3932160 | tf_op jit(solution)/shard_map/reshape | solution.py:82
  106.8 0.0 all-gather.3.cloned.1.call-update
  106.8 0.0 copy-done.2
  106.8 0.0 slice-start.2
  106.8 5.3 %fusion.6 = f32[640,1536]{1,0:T(8,128)S(1)} fusion(bf16[640,1536]{1,0:T(8,128)(2,1)S(1)} %copy-done.2, bf16[1,1536,1536]{2,1,0:T(8,128)(2,1)} %param.16), kind=kOutput, calls=%fused_computation.6 | convolution fusion | flops 3019898880 | bytes 10616832 | tf_op jit(solution)/shard_map/dot_general | solution.py:10
  112.1 0.0 copy-start.11
  112.1 0.0 copy-start.3
  112.1 0.0 slice-start.3
  112.1 6.6 %fusion.2 = f32[640,1536]{1,0:T(8,128)S(1)} fusion(bf16[640,1536]{1,0:T(8,128)(2,1)S(1)} %copy-done.2, bf16[1,1536,1536]{2,1,0:T(8,128)(2,1)} %param.15), kind=kOutput, calls=%fused_computation.2 | convolution fusion | flops 3019898880 | bytes 10616832 | tf_op jit(solution)/shard_map/dot_general | solution.py:10
  118.8 0.0 copy-done.11
  118.8 0.0 slice-done.2
  118.8 0.0 copy-done.3
  118.8 5.4 %multiply_reduce_fusion = (bf16[640]{0:T(1024)(128)(2,1)S(1)}, f32[640,1536]{1,0:T(8,128)}) fusion(f32[640,1536]{1,0:T(8,128)S(1)} %fusion.6, f32[640,1536]{1,0:T(8,128)S(1)} %fusion.2, bf16[640,1536]{1,0:T(8,128)(2,1)S(1)} %copy-done.3, bf16[1,1536,1536]{2,1,0:T(8,128)(2,1)S(1)} %bitcast.64), kind=kOutput, calls=%fused_computation.15 | convolution fusion | flops 3028745728 | bytes 18482432 | tf_op jit(solution)/shard_map/dot_general | solution.py:10
  124.2 0.0 copy-done.9
  124.2 0.7 convert_element_type.97
  124.9 3.8 %all-to-all-start.3 = ((bf16[32,1,20]{2,1,0:T(2,128)(2,1)}), bf16[32,1,20]{2,1,0:T(2,128)(2,1)S(1)}, u32[]{:S(2)}, u32[]{:S(2)}) async-start(bf16[32,1,20]{2,1,0:T(2,128)(2,1)} %convert_element_type.97), calls=%async_computation.3 | async-start | bytes 32768 | tf_op jit(solution)/shard_map/all_to_all | solution.py:78
  128.8 0.0 copy-start.10
  128.8 0.0 copy-start.13
  128.8 8.9 %fusion = f32[640,1536]{1,0:T(8,128)S(1)} fusion(bf16[1,1536,1536]{2,1,0:T(8,128)(2,1)} %param.15, f32[640,1536]{1,0:T(8,128)} %get-tuple-element.12, f32[640,1536]{1,0:T(8,128)} %copy-done.9, f32[640,1536]{1,0:T(8,128)} %copy-done.11), kind=kOutput, calls=%fused_computation | convolution fusion | flops 3031695360 | bytes 20447232 | tf_op jit(solution)/shard_map/dot_general | solution.py:89
  137.7 5.8 %add_convert_fusion = bf16[640,1536]{1,0:T(8,128)(2,1)S(1)} fusion(f32[640,1536]{1,0:T(8,128)S(1)} %fusion, bf16[1,1536,1536]{2,1,0:T(8,128)(2,1)} %param.16, f32[640,1536]{1,0:T(8,128)S(1)} %copy-done.13, f32[640,1536]{1,0:T(8,128)S(1)} %copy-done.10), kind=kOutput, calls=%fused_computation.16 | convolution fusion | flops 3028746240 | bytes 18481152 | tf_op jit(solution)/shard_map/dot_general | solution.py:90
  143.6 0.0 copy-start.5
  143.6 2.1 reshape.96
  145.7 0.0 all-to-all-done.3
  145.7 7.3 %all-to-all-start.2 = ((bf16[32,20,1536]{2,1,0:T(8,128)(2,1)}), bf16[32,20,1536]{2,1,0:T(8,128)(2,1)S(1)}, u32[]{:S(2)}, u32[]{:S(2)}) async-start(bf16[32,20,1536]{2,1,0:T(8,128)(2,1)} %reshape.96), calls=%async_computation.2 | async-start | bytes 4718592 | tf_op jit(solution)/shard_map/all_to_all | solution.py:78
  153.0 0.1 copy.33
  153.1 0.2 fusion.17
  153.4 0.6 div.20
  154.0 30.6 %all-to-all-done.2 = bf16[32,20,1536]{2,1,0:T(8,128)(2,1)S(1)} async-done(((bf16[32,20,1536]{2,1,0:T(8,128)(2,1)}), bf16[32,20,1536]{2,1,0:T(8,128)(2,1)S(1)}, u32[]{:S(2)}, u32[]{:S(2)}) %all-to-all-start.2) | async-done | bytes 1966112 | tf_op jit(solution)/shard_map/all_to_all | solution.py:78
  184.5 1.5 fusion.19
  186.1 9.9 %fusion.25 = f32[2560,384]{1,0:T(8,128)} fusion(bf16[2560,1536]{1,0:T(8,128)(2,1)} %all-gather.5.cloned.1.call-done, bf16[1,1536,1536]{2,1,0:T(8,128)(2,1)} %param.15, s32[]{:T(128)S(6)} %select_n.2), kind=kOutput, calls=%fused_computation.41 | convolution fusion | flops 3019898880 | bytes 12976132 | tf_op jit(solution)/shard_map/dot_general | solution.py:10
  196.0 0.0 copy-done.6
  196.0 7.5 %convolution_add_fusion = f32[2560,384]{1,0:T(8,128)} fusion(bf16[2560,1536]{1,0:T(8,128)(2,1)S(1)} %copy-done.6, bf16[1,1536,1536]{2,1,0:T(8,128)(2,1)} %param.16, s32[]{:T(128)S(6)} %select_n.2), kind=kOutput, calls=%fused_computation.10 | convolution fusion | flops 3020881920 | bytes 12976132 | tf_op jit(solution)/shard_map/dot_general | solution.py:10
  203.4 16.9 %all-gather.3.cloned.1.call-done = bf16[2560,1536]{1,0:T(8,128)(2,1)} async-done(((bf16[640,1536]{1,0:T(8,128)(2,1)}), bf16[2560,1536]{1,0:T(8,128)(2,1)}) %all-gather.3.cloned.1.call-update) | async-done | bytes 7864336 | tf_op jit(solution)/shard_map/all_gather | solution.py:83
  220.3 7.4 %fusion.28 = f32[2560,384]{1,0:T(8,128)S(1)} fusion(bf16[2560,1536]{1,0:T(8,128)(2,1)} %all-gather.3.cloned.1.call-done, bf16[1,1536,1536]{2,1,0:T(8,128)(2,1)} %param.17, s32[]{:T(128)S(6)} %select_n.2), kind=kOutput, calls=%fused_computation.44 | convolution fusion | flops 3019898880 | bytes 12976132 | tf_op jit(solution)/shard_map/dot_general | solution.py:10
  227.7 0.0 slice-start
  227.7 4.4 %fusion.15 = bf16[1,384,1536]{2,1,0:T(8,128)(2,1)} fusion(bf16[2560,1536]{1,0:T(8,128)(2,1)S(1)} %copy-done.7, f32[2560,384]{1,0:T(8,128)S(1)} %fusion.28, f32[2560,384]{1,0:T(8,128)S(1)} %copy-done.8), kind=kOutput, calls=%fused_computation.28 | convolution fusion | flops 3027369984 | bytes 16908288 | tf_op jit(solution)/shard_map/dot_general | solution.py:16
  232.2 0.0 copy-done.12
  232.2 4.5 %fusion.14 = bf16[1,384,1536]{2,1,0:T(8,128)(2,1)} fusion(bf16[2560,1536]{1,0:T(8,128)(2,1)S(1)} %copy-done.7, f32[2560,384]{1,0:T(8,128)S(1)} %fusion.28, f32[2560,384]{1,0:T(8,128)S(1)} %copy-done.12, f32[2560,384]{1,0:T(8,128)S(1)} %copy-done.8), kind=kOutput, calls=%fused_computation.27 | convolution fusion | flops 3031302144 | bytes 20840448 | tf_op jit(solution)/shard_map/dot_general | solution.py:16
  236.7 0.0 slice-done.1
  236.7 4.4 %fusion.16 = bf16[1,384,1536]{2,1,0:T(8,128)(2,1)} fusion(bf16[2560,1536]{1,0:T(8,128)(2,1)S(1)} %bitcast.62, f32[2560,384]{1,0:T(8,128)S(1)} %copy-done.12, f32[2560,384]{1,0:T(8,128)S(1)} %copy-done.8), kind=kOutput, calls=%fused_computation.29 | convolution fusion | flops 3027369984 | bytes 16908288 | tf_op jit(solution)/shard_map/dot_general | solution.py:16
  (25 shorter events, 0.1 us)
Async XLA Ops:
  7.2 6.5 %copy-start = (bf16[128,1536]{1,0:T(8,128)(2,1)S(1)}, bf16[128,1536]{1,0:T(8,128)(2,1)}, u32[]{:S(2)}) copy-start(bf16[128,1536]{1,0:T(8,128)(2,1)} %param.10) | copy-start | bytes 1179652
  7.2 178.9 %all-gather.5.cloned.1.call-start = ((), (), s32[]{:S(2)}) async-start(), calls=%async_computation.5 | async-start | bytes 9830400 | tf_op jit(solution)/shard_map/all_gather | solution.py:81
  58.7 4.3 %copy-start.4 = (f32[128,1536]{1,0:T(8,128)S(1)}, f32[128,1536]{1,0:T(8,128)}, u32[]{:S(2)}) copy-start(f32[128,1536]{1,0:T(8,128)} %param.9) | copy-start | bytes 2359300
  62.8 157.5 %all-gather.3.cloned.1.call-start = ((), (), s32[]{:S(2)}) async-start(), calls=%async_computation.4 | async-start | bytes 9830400 | tf_op jit(solution)/shard_map/all_gather | solution.py:83
  102.6 4.2 %copy-start.2 = (bf16[640,1536]{1,0:T(8,128)(2,1)S(1)}, bf16[640,1536]{1,0:T(8,128)(2,1)}, u32[]{:S(2)}) copy-start(bf16[640,1536]{1,0:T(8,128)(2,1)} %reshape.95) | copy-start | bytes 5898244
  106.8 12.0 %slice-start.2 = ((s8[4718592]{0:T(1024)(128)(4,1)}), s8[4194304]{0:T(1024)(128)(4,1)S(1)}, s32[]{:S(2)}) async-start(s8[4718592]{0:T(1024)(128)(4,1)} %bitcast.63), calls=%async_computation.8 | async-start | bytes 8388608
  112.1 6.7 %copy-start.11 = (f32[640,1536]{1,0:T(8,128)}, f32[640,1536]{1,0:T(8,128)S(1)}, u32[]{:S(2)}) copy-start(f32[640,1536]{1,0:T(8,128)S(1)} %fusion.6) | copy-start | bytes 11796484
  112.1 6.7 %copy-start.3 = (bf16[640,1536]{1,0:T(8,128)(2,1)S(1)}, bf16[640,1536]{1,0:T(8,128)(2,1)}, u32[]{:S(2)}) copy-start(bf16[640,1536]{1,0:T(8,128)(2,1)} %reshape.93) | copy-start | bytes 5898244
  112.1 6.7 %slice-start.3 = ((s8[4718592]{0:T(1024)(128)(4,1)}), s8[524288]{0:T(1024)(128)(4,1)S(1)}, s32[]{:S(2)}) async-start(s8[4718592]{0:T(1024)(128)(4,1)} %bitcast.63), calls=%async_computation.9 | async-start | bytes 1048576
  118.8 5.4 %copy-start.9 = (f32[640,1536]{1,0:T(8,128)}, f32[640,1536]{1,0:T(8,128)S(1)}, u32[]{:S(2)}) copy-start(f32[640,1536]{1,0:T(8,128)S(1)} %fusion.2) | copy-start | bytes 11796484
  124.9 20.7 %all-to-all-start.3 = ((bf16[32,1,20]{2,1,0:T(2,128)(2,1)}), bf16[32,1,20]{2,1,0:T(2,128)(2,1)S(1)}, u32[]{:S(2)}, u32[]{:S(2)}) async-start(bf16[32,1,20]{2,1,0:T(2,128)(2,1)} %convert_element_type.97), calls=%async_computation.3 | async-start | bytes 32768 | tf_op jit(solution)/shard_map/all_to_all | solution.py:78
  128.8 9.0 %copy-start.10 = (f32[640,1536]{1,0:T(8,128)S(1)}, f32[640,1536]{1,0:T(8,128)}, u32[]{:S(2)}) copy-start(f32[640,1536]{1,0:T(8,128)} %copy-done.9) | copy-start | bytes 11796484
  128.8 9.0 %copy-start.13 = (f32[640,1536]{1,0:T(8,128)S(1)}, f32[640,1536]{1,0:T(8,128)}, u32[]{:S(2)}) copy-start(f32[640,1536]{1,0:T(8,128)} %get-tuple-element.12) | copy-start | bytes 11796484
  143.6 9.8 %copy-start.5 = (f32[128,4]{0,1:T(4,128)S(1)}, f32[128,4]{0,1:T(4,128)}, u32[]{:S(2)}) copy-start(f32[128,4]{0,1:T(4,128)} %param.11) | copy-start | bytes 6148
  145.7 38.9 %all-to-all-start.2 = ((bf16[32,20,1536]{2,1,0:T(8,128)(2,1)}), bf16[32,20,1536]{2,1,0:T(8,128)(2,1)S(1)}, u32[]{:S(2)}, u32[]{:S(2)}) async-start(bf16[32,20,1536]{2,1,0:T(8,128)(2,1)} %reshape.96), calls=%async_computation.2 | async-start | bytes 4718592 | tf_op jit(solution)/shard_map/all_to_all | solution.py:78
  186.1 9.9 %copy-start.6 = (bf16[2560,1536]{1,0:T(8,128)(2,1)S(1)}, bf16[2560,1536]{1,0:T(8,128)(2,1)}, u32[]{:S(2)}) copy-start(bf16[2560,1536]{1,0:T(8,128)(2,1)} %all-gather.5.cloned.1.call-done) | copy-start | bytes 23592964
  220.3 7.4 %copy-start.7 = (bf16[2560,1536]{1,0:T(8,128)(2,1)S(1)}, bf16[2560,1536]{1,0:T(8,128)(2,1)}, u32[]{:S(2)}) copy-start(bf16[2560,1536]{1,0:T(8,128)(2,1)} %all-gather.5.cloned.1.call-done) | copy-start | bytes 23592964
  220.3 7.4 %copy-start.8 = (f32[2560,384]{1,0:T(8,128)S(1)}, f32[2560,384]{1,0:T(8,128)}, u32[]{:S(2)}) copy-start(f32[2560,384]{1,0:T(8,128)} %fusion.25) | copy-start | bytes 11796484
  227.7 4.5 %copy-start.12 = (f32[2560,384]{1,0:T(8,128)S(1)}, f32[2560,384]{1,0:T(8,128)}, u32[]{:S(2)}) copy-start(f32[2560,384]{1,0:T(8,128)} %convolution_add_fusion) | copy-start | bytes 11796484
  227.7 9.0 %slice-start = ((s8[7864320]{0:T(1024)(128)(4,1)}), s8[4194304]{0:T(1024)(128)(4,1)S(1)}, s32[]{:S(2)}) async-start(s8[7864320]{0:T(1024)(128)(4,1)} %bitcast.61), calls=%async_computation.6 | async-start | bytes 8388608
  232.2 4.6 %slice-start.1 = ((s8[7864320]{0:T(1024)(128)(4,1)}), s8[3670016]{0:T(1024)(128)(4,1)S(1)}, s32[]{:S(2)}) async-start(s8[7864320]{0:T(1024)(128)(4,1)} %bitcast.61), calls=%async_computation.7 | async-start | bytes 7340032
  236.7 4.4 %copy-start.1 = (bf16[128,1536]{1,0:T(8,128)(2,1)S(1)}, bf16[128,1536]{1,0:T(8,128)(2,1)}, u32[]{:S(2)}) copy-start(bf16[128,1536]{1,0:T(8,128)(2,1)} %param.10) | copy-start | bytes 1179652
Sparse Core Ops, SparseCore 0:
  62.9 76.0 all-gather.4
  140.7 79.5 all-gather.2
where the time goes:
time: 249 us; the launch traced here: 248 us
  matrix products  76.9 us (31%)
  blocking collectives  75.7 us (30%)
  waiting for transfers between devices  47.5 us (19%)
  local copies, waits for them, and re-layouts  16.4 us (7%)
  between operations  14.4 us (6%)
  starting transfers between devices  11.2 us (4%)
  other arithmetic  5.9 us (2%)
    all_to_all x2, blocking collectives, exchange(): return lax.all_to_all(a, 'ep', split_axis=0, concat_axis=0, tiled=True)  75.7 us
    dot_general x6, matrix products, contract_last(): lax.dot_general(first_op, second_op, (((1,), (1,)), ((), ())), preferred_...  42 us
    all_to_all x2, waiting for transfers between devices, exchange(): return lax.all_to_all(a, 'ep', split_axis=0, concat_axis=0, tiled=True)  30.6 us
    all_gather x1, waiting for transfers between devices, on_device(): all_g = lax.all_gather(slot_g, 'dp', axis=0, tiled=True)  16.9 us
    dot_general x3, matrix products, contract_first(): lax.dot_general(first_op, second_op, (((0,), (0,)), ((), ())), preferred_...  13.4 us
    all_to_all x2, starting transfers between devices, exchange(): return lax.all_to_all(a, 'ep', split_axis=0, concat_axis=0, tiled=True)  11.1 us
    dot_general x1, matrix products, on_device(): jnp.dot(gate_delta, w_gate, preferred_element_type=jnp.float32)  8.95 us
    dot_general x1, matrix products, on_device(): jnp.dot(up_delta, w_up, preferred_element_type=jnp.float32)  5.8 us
  transfers between devices with their start and end apart: 4, of which 2 were waited for; matrix products, arithmetic and copies ran while one was open for 26% of the time, Pallas kernels for 0%

commit v1 on v0

--- a/solution.py
+++ b/solution.py
@@ -80,7 +80,23 @@
     slot_x = exchange(send_x.reshape(bucket_shape)).reshape(slot_rows, model_width)
     all_x = lax.all_gather(slot_x, "dp", axis=0, tiled=True)
     slot_g = exchange(send_g.reshape(bucket_shape)).reshape(slot_rows, model_width)
-    all_g = lax.all_gather(slot_g, "dp", axis=0, tiled=True)
+    size, here, rows = (lax.axis_size("dp"), lax.axis_index("dp"), slot_g.shape[0])
+    right = [(i, (i + 1) % size) for i in range(size)]
+    behind = [(i, (i - 1) % size) for i in range(size)]
+    all_g = jnp.zeros((*slot_g.shape[:0], size * rows, *slot_g.shape[0 + 1 :]), slot_g.dtype)
+    all_g = lax.dynamic_update_slice_in_dim(all_g, slot_g, here * rows, axis=0)
+    from_left = from_right = slot_g
+    halfway = size // 2
+    for step in range(1, halfway + 1):
+        from_left = lax.ppermute(from_left, "dp", right)
+        all_g = lax.dynamic_update_slice_in_dim(
+            all_g, from_left, (here - step) % size * rows, axis=0
+        )
+        if step < size - halfway:
+            from_right = lax.ppermute(from_right, "dp", behind)
+            all_g = lax.dynamic_update_slice_in_dim(
+                all_g, from_right, (here + step) % size * rows, axis=0
+            )
     w_gate = gate_weight[0]
     w_up = up_weight[0]
     w_down = down_weight[0]

time: 249 us -> 275 us (1.10)
  waiting for transfers between devices: 47.5 us -> 87 us
  blocking collectives: 75.7 us -> 36.7 us
  starting transfers between devices: 11.2 us -> 23.6 us
  local copies, waits for them, and re-layouts: 16.4 us -> 27.8 us
    ppermute x0 -> x3, waiting for transfers between devices: none -> 55.2 us  [the longest x2 46.7 us: on_device(): from_left = lax.ppermute(from_left, 'dp', right)]
    all_to_all x2 -> x1, blocking collectives: 75.7 us -> 36.7 us  [exchange(): return lax.all_to_all(a, 'ep', split_axis=0, concat_axis=0, tiled=True)]
    all_gather x1 -> x0, waiting for transfers between devices: 16.9 us -> none  [on_device(): all_g = lax.all_gather(slot_g, 'dp', axis=0, tiled=True)]
    dynamic_update_slice x0 -> x4, local copies, waits for them, and re-layouts: none -> 10.3 us  [the longest x2 5.95 us: on_device(): lax.dynamic_update_slice_in_dim(all_g, from_left, (here - step) % size *...]
    all_to_all x2 -> x3, starting transfers between devices: 11.1 us -> 20.9 us  [exchange(): return lax.all_to_all(a, 'ep', split_axis=0, concat_axis=0, tiled=True)]
    broadcast_in_dim x0 -> x1, local copies, waits for them, and re-layouts: none -> 3.58 us  [on_device(): jnp.zeros((*slot_g.shape[:0], size * rows, *slot_g.shape[0 + 1:]), slot_g...]
    dot_general x3, matrix products: 13.4 us -> 16.9 us  [contract_first(): lax.dot_general(first_op, second_op, (((0,), (0,)), ((), ())), preferred_...]
    all_to_all x2 -> x3, waiting for transfers between devices: 30.6 us -> 31.7 us  [exchange(): return lax.all_to_all(a, 'ep', split_axis=0, concat_axis=0, tiled=True)]
  transfers between devices with their start and end apart: 4 -> 7, of which waited for: 2 -> 5; matrix products, arithmetic and copies ran while one was open for 26% -> 26% of each run, Pallas kernels for 0% -> 0%
where the time goes in v1:
time: 275 us; the launch traced here: 274 us
  waiting for transfers between devices  87 us (32%)
  matrix products  78.5 us (29%)
  blocking collectives  36.7 us (13%)
  local copies, waits for them, and re-layouts  27.8 us (10%)
  starting transfers between devices  23.6 us (9%)
  between operations  14.3 us (5%)
  other arithmetic  5.91 us (2%)
    ppermute x2, waiting for transfers between devices, on_device(): from_left = lax.ppermute(from_left, 'dp', right)  46.7 us
    dot_general x6, matrix products, contract_last(): lax.dot_general(first_op, second_op, (((1,), (1,)), ((), ())), preferred_...  40.3 us
    all_to_all x1, blocking collectives, exchange(): return lax.all_to_all(a, 'ep', split_axis=0, concat_axis=0, tiled=True)  36.7 us
    all_to_all x3, waiting for transfers between devices, exchange(): return lax.all_to_all(a, 'ep', split_axis=0, concat_axis=0, tiled=True)  31.7 us
    all_to_all x3, starting transfers between devices, exchange(): return lax.all_to_all(a, 'ep', split_axis=0, concat_axis=0, tiled=True)  20.9 us
    dot_general x3, matrix products, contract_first(): lax.dot_general(first_op, second_op, (((0,), (0,)), ((), ())), preferred_...  16.9 us
    dot_general x1, matrix products, on_device(): jnp.dot(gate_delta, w_gate, preferred_element_type=jnp.float32)  8.94 us
    ppermute x1, waiting for transfers between devices, on_device(): from_right = lax.ppermute(from_right, 'dp', behind)  8.51 us
  transfers between devices with their start and end apart: 7, of which 5 were waited for; matrix products, arithmetic and copies ran while one was open for 26% of the time, Pallas kernels for 0%

profile of v1, /device:TPU:1, one launch (start us, length us, event | category | flops | bytes accessed | tf_op | source)
XLA Modules:
  0.0 273.9 jit_solution(18420180064385169163)
XLA Ops:
  7.2 0.0 copy-start
  7.2 0.7 convert_element_type.78
  7.9 0.7 fusion.39
  8.6 0.8 select_reduce_fusion
  9.4 0.9 fusion.40
  10.3 0.7 select_reduce_fusion.1
  11.0 1.3 abs_reduce_fusion
  12.3 1.0 fusion.24
  13.3 0.2 multiply_reduce_fusion.2
  13.5 0.1 copy.29
  13.6 0.0 copy-done
  13.6 0.7 convolution_convert_fusion
  14.2 2.1 reshape.94
  16.3 9.4 %all-to-all-start.1 = ((bf16[32,20,1536]{2,1,0:T(8,128)(2,1)}), bf16[32,20,1536]{2,1,0:T(8,128)(2,1)S(1)}, u32[]{:S(2)}, u32[]{:S(2)}) async-start(bf16[32,20,1536]{2,1,0:T(8,128)(2,1)} %reshape.94), calls=%async_computation.1 | async-start | bytes 4718592 | tf_op jit(solution)/shard_map/all_to_all | solution.py:78
  25.8 0.0 all-gather.2.cloned.1.call-start
  25.8 0.1 copy.30
  25.9 0.1 mul.148
  26.0 31.3 %all-to-all-done.1 = bf16[32,20,1536]{2,1,0:T(8,128)(2,1)S(1)} async-done(((bf16[32,20,1536]{2,1,0:T(8,128)(2,1)}), bf16[32,20,1536]{2,1,0:T(8,128)(2,1)S(1)}, u32[]{:S(2)}, u32[]{:S(2)}) %all-to-all-start.1) | async-done | bytes 1966112 | tf_op jit(solution)/shard_map/all_to_all | solution.py:78
  57.3 2.1 reshape.95
  59.3 0.0 all-gather.2.cloned.1.call-update
  59.4 3.1 %multiply_convert_fusion.5 = bf16[640,1536]{1,0:T(8,128)(2,1)} fusion(bf16[128,640]{0,1:T(8,128)(2,1)S(1)} %convert_element_type.81, f32[640]{0:T(1024)S(1)} %mul.148, f32[128,1536]{1,0:T(8,128)} %param.9, f32[128]{0:T(128)S(1)} %broadcast_maximum_fusion), kind=kOutput, calls=%fused_computation.20 | convolution fusion | flops 254017536 | bytes 2919424 | tf_op jit(solution)/shard_map/ts,td->sd/dot_general | solution.py:72
  62.5 2.5 reshape.92
  65.0 36.7 %all_to_all.24 = bf16[32,20,1536]{2,1,0:T(8,128)(2,1)} all-to-all(bf16[32,20,1536]{2,1,0:T(8,128)(2,1)S(1)} %reshape.92), channel_id=1, replica_groups=mesh['ep'=32,'dp'=4] {'ep'}, dimensions={0} | all-to-all | bytes 3932160 | tf_op jit(solution)/shard_map/all_to_all | solution.py:78
  101.7 4.1 %reshape.93 = bf16[640,1536]{1,0:T(8,128)(2,1)} reshape(bf16[32,20,1536]{2,1,0:T(8,128)(2,1)} %all_to_all.24) | data formatting | bytes 3932160 | tf_op jit(solution)/shard_map/reshape | solution.py:82
  105.7 1.3 collective-permute-start
  107.0 5.3 %fusion.6 = f32[640,1536]{1,0:T(8,128)S(1)} fusion(bf16[640,1536]{1,0:T(8,128)(2,1)S(1)} %copy-done.2, bf16[1,1536,1536]{2,1,0:T(8,128)(2,1)} %param.16), kind=kOutput, calls=%fused_computation.6 | convolution fusion | flops 3019898880 | bytes 10616832 | tf_op jit(solution)/shard_map/dot_general | solution.py:10
  112.4 0.0 slice-start.1
  112.4 6.6 %fusion.2 = f32[640,1536]{1,0:T(8,128)S(1)} fusion(bf16[640,1536]{1,0:T(8,128)(2,1)S(1)} %copy-done.2, bf16[1,1536,1536]{2,1,0:T(8,128)(2,1)} %param.15), kind=kOutput, calls=%fused_computation.2 | convolution fusion | flops 3019898880 | bytes 10616832 | tf_op jit(solution)/shard_map/dot_general | solution.py:10
  119.0 5.3 %multiply_reduce_fusion = (bf16[640]{0:T(1024)(128)(2,1)S(1)}, f32[640,1536]{1,0:T(8,128)}) fusion(f32[640,1536]{1,0:T(8,128)S(1)} %fusion.6, f32[640,1536]{1,0:T(8,128)S(1)} %fusion.2, bf16[640,1536]{1,0:T(8,128)(2,1)S(1)} %copy-done.3, bf16[1,1536,1536]{2,1,0:T(8,128)(2,1)S(1)} %bitcast.62), kind=kOutput, calls=%fused_computation.15 | convolution fusion | flops 3028745728 | bytes 18482432 | tf_op jit(solution)/shard_map/dot_general | solution.py:10
  124.4 0.0 copy-done.8
  124.4 0.7 convert_element_type.97
  125.1 4.0 %all-to-all-start.3 = ((bf16[32,1,20]{2,1,0:T(2,128)(2,1)}), bf16[32,1,20]{2,1,0:T(2,128)(2,1)S(1)}, u32[]{:S(2)}, u32[]{:S(2)}) async-start(bf16[32,1,20]{2,1,0:T(2,128)(2,1)} %convert_element_type.97), calls=%async_computation.3 | async-start | bytes 32768 | tf_op jit(solution)/shard_map/all_to_all | solution.py:78
  129.1 0.0 copy-start.9
  129.2 0.0 copy-start.11
  129.2 8.9 %fusion = f32[640,1536]{1,0:T(8,128)S(1)} fusion(bf16[1,1536,1536]{2,1,0:T(8,128)(2,1)} %param.15, f32[640,1536]{1,0:T(8,128)} %get-tuple-element.12, f32[640,1536]{1,0:T(8,128)} %copy-done.8, f32[640,1536]{1,0:T(8,128)} %copy-done.10), kind=kOutput, calls=%fused_computation | convolution fusion | flops 3031695360 | bytes 20447232 | tf_op jit(solution)/shard_map/dot_general | solution.py:105
  138.1 0.0 copy-done.9
  138.1 0.0 copy-done.11
  138.1 5.8 %add_convert_fusion = bf16[640,1536]{1,0:T(8,128)(2,1)S(1)} fusion(f32[640,1536]{1,0:T(8,128)S(1)} %fusion, bf16[1,1536,1536]{2,1,0:T(8,128)(2,1)} %param.16, f32[640,1536]{1,0:T(8,128)S(1)} %copy-done.11, f32[640,1536]{1,0:T(8,128)S(1)} %copy-done.9), kind=kOutput, calls=%fused_computation.16 | convolution fusion | flops 3028746240 | bytes 18481152 | tf_op jit(solution)/shard_map/dot_general | solution.py:106
  143.9 2.1 reshape.96
  146.1 0.0 all-to-all-done.3
  146.1 7.4 %all-to-all-start.2 = ((bf16[32,20,1536]{2,1,0:T(8,128)(2,1)}), bf16[32,20,1536]{2,1,0:T(8,128)(2,1)S(1)}, u32[]{:S(2)}, u32[]{:S(2)}) async-start(bf16[32,20,1536]{2,1,0:T(8,128)(2,1)} %reshape.96), calls=%async_computation.2 | async-start | bytes 4718592 | tf_op jit(solution)/shard_map/all_to_all | solution.py:78
  153.5 1.4 collective-permute-start.1
  154.9 23.7 %collective-permute-done = bf16[640,1536]{1,0:T(8,128)(2,1)} collective-permute-done((bf16[640,1536]{1,0:T(8,128)(2,1)}, bf16[640,1536]{1,0:T(8,128)(2,1)}, u32[]{:S(2)}, u32[]{:S(2)}) %collective-permute-start) | collective-permute-done | bytes 1966112 | tf_op jit(solution)/shard_map/ppermute | solution.py:91
  178.6 0.0 collective-permute-start.2
  178.6 3.6 %broadcast_in_dim.8 = bf16[2560,1536]{1,0:T(8,128)(2,1)} broadcast(bf16[]{:T(256)} %constant.47.clone.1), dimensions={} | broadcast | bytes 7864322 | tf_op jit(solution)/shard_map/broadcast_in_dim | solution.py:86
  182.2 0.0 copy-done.4
  182.2 1.4 constant_dynamic-update-slice_fusion.3
  183.6 0.1 copy.33
  183.7 0.2 fusion.17
  183.9 0.0 copy-done.5
  183.9 0.6 div.20
  184.5 0.5 all-to-all-done.2
  185.0 1.5 fusion.19
  186.5 3.0 %constant_dynamic-update-slice_fusion.2 = bf16[2560,1536]{1,0:T(8,128)(2,1)} fusion(bf16[2560,1536]{1,0:T(8,128)(2,1)} %constant_dynamic-update-slice_fusion.3, bf16[640,1536]{1,0:T(8,128)(2,1)} %collective-permute-done, s32[]{:T(128)S(6)} %select_n.34), kind=kLoop, calls=%fused_computation.73 | loop fusion | bytes 3932164 | tf_op jit(solution)/shard_map/dynamic_update_slice | solution.py:92
  189.5 8.5 %collective-permute-done.1 = bf16[640,1536]{1,0:T(8,128)(2,1)} collective-permute-done((bf16[640,1536]{1,0:T(8,128)(2,1)}, bf16[640,1536]{1,0:T(8,128)(2,1)}, u32[]{:S(2)}, u32[]{:S(2)}) %collective-permute-start.1) | collective-permute-done | bytes 1966112 | tf_op jit(solution)/shard_map/ppermute | solution.py:96
  198.0 2.9 %constant_dynamic-update-slice_fusion.1 = bf16[2560,1536]{1,0:T(8,128)(2,1)} fusion(bf16[2560,1536]{1,0:T(8,128)(2,1)} %constant_dynamic-update-slice_fusion.2, bf16[640,1536]{1,0:T(8,128)(2,1)} %collective-permute-done.1, s32[]{:T(128)S(6)} %select_n.36), kind=kLoop, calls=%fused_computation.72 | loop fusion | bytes 3932164 | tf_op jit(solution)/shard_map/dynamic_update_slice | solution.py:97
  200.9 23.0 %collective-permute-done.2 = bf16[640,1536]{1,0:T(8,128)(2,1)} collective-permute-done((bf16[640,1536]{1,0:T(8,128)(2,1)}, bf16[640,1536]{1,0:T(8,128)(2,1)}, u32[]{:S(2)}, u32[]{:S(2)}) %collective-permute-start.2) | collective-permute-done | bytes 1966112 | tf_op jit(solution)/shard_map/ppermute | solution.py:91
  224.0 3.0 %constant_dynamic-update-slice_fusion = bf16[2560,1536]{1,0:T(8,128)(2,1)} fusion(bf16[2560,1536]{1,0:T(8,128)(2,1)} %constant_dynamic-update-slice_fusion.1, bf16[640,1536]{1,0:T(8,128)(2,1)} %collective-permute-done.2, s32[]{:T(128)S(6)} %select_n.38), kind=kLoop, calls=%fused_computation.71 | loop fusion | bytes 3932164 | tf_op jit(solution)/shard_map/dynamic_update_slice | solution.py:92
  227.0 9.8 %fusion.28 = f32[2560,384]{1,0:T(8,128)} fusion(bf16[2560,1536]{1,0:T(8,128)(2,1)} %constant_dynamic-update-slice_fusion, bf16[1,1536,1536]{2,1,0:T(8,128)(2,1)} %param.17, s32[]{:T(128)S(6)} %select_n.39), kind=kOutput, calls=%fused_computation.44 | convolution fusion | flops 3019898880 | bytes 12976132 | tf_op jit(solution)/shard_map/dot_general | solution.py:10
  236.8 7.7 %convolution_add_fusion = f32[2560,384]{1,0:T(8,128)S(1)} fusion(bf16[2560,1536]{1,0:T(8,128)(2,1)} %all-gather.2.cloned.1.call-done, bf16[1,1536,1536]{2,1,0:T(8,128)(2,1)} %param.16, s32[]{:T(128)S(6)} %select_n.39), kind=kOutput, calls=%fused_computation.10 | convolution fusion | flops 3020881920 | bytes 12976132 | tf_op jit(solution)/shard_map/dot_general | solution.py:10
  244.5 5.6 %fusion.25 = f32[2560,384]{1,0:T(8,128)S(1)} fusion(bf16[2560,1536]{1,0:T(8,128)(2,1)S(1)} %copy-done.6, bf16[1,1536,1536]{2,1,0:T(8,128)(2,1)} %param.15, s32[]{:T(128)S(6)} %select_n.39), kind=kOutput, calls=%fused_computation.41 | convolution fusion | flops 3019898880 | bytes 12976132 | tf_op jit(solution)/shard_map/dot_general | solution.py:10
  250.1 7.9 %fusion.16 = bf16[1,384,1536]{2,1,0:T(8,128)(2,1)} fusion(bf16[2560,1536]{1,0:T(8,128)(2,1)} %constant_dynamic-update-slice_fusion, f32[2560,384]{1,0:T(8,128)S(1)} %convolution_add_fusion, f32[2560,384]{1,0:T(8,128)S(1)} %fusion.25), kind=kOutput, calls=%fused_computation.29 | convolution fusion | flops 3027369984 | bytes 16908288 | tf_op jit(solution)/shard_map/dot_general | solution.py:16
  258.0 4.5 %fusion.14 = bf16[1,384,1536]{2,1,0:T(8,128)(2,1)} fusion(bf16[2560,1536]{1,0:T(8,128)(2,1)S(1)} %copy-done.6, f32[2560,384]{1,0:T(8,128)S(1)} %copy-done.7, f32[2560,384]{1,0:T(8,128)S(1)} %convolution_add_fusion, f32[2560,384]{1,0:T(8,128)S(1)} %fusion.25), kind=kOutput, calls=%fused_computation.27 | convolution fusion | flops 3031302144 | bytes 20840448 | tf_op jit(solution)/shard_map/dot_general | solution.py:16
  262.6 4.4 %fusion.15 = bf16[1,384,1536]{2,1,0:T(8,128)(2,1)} fusion(bf16[2560,1536]{1,0:T(8,128)(2,1)S(1)} %copy-done.6, f32[2560,384]{1,0:T(8,128)S(1)} %copy-done.7, f32[2560,384]{1,0:T(8,128)S(1)} %fusion.25), kind=kOutput, calls=%fused_computation.28 | convolution fusion | flops 3027369984 | bytes 16908288 | tf_op jit(solution)/shard_map/dot_general | solution.py:16
  (25 shorter events, 0.1 us)
Async XLA Ops:
  7.2 6.4 %copy-start = (bf16[128,1536]{1,0:T(8,128)(2,1)S(1)}, bf16[128,1536]{1,0:T(8,128)(2,1)}, u32[]{:S(2)}) copy-start(bf16[128,1536]{1,0:T(8,128)(2,1)} %param.10) | copy-start | bytes 1179652
  16.3 40.9 %all-to-all-start.1 = ((bf16[32,20,1536]{2,1,0:T(8,128)(2,1)}), bf16[32,20,1536]{2,1,0:T(8,128)(2,1)S(1)}, u32[]{:S(2)}, u32[]{:S(2)}) async-start(bf16[32,20,1536]{2,1,0:T(8,128)(2,1)} %reshape.94), calls=%async_computation.1 | async-start | bytes 4718592 | tf_op jit(solution)/shard_map/all_to_all | solution.py:78
  25.8 211.0 %all-gather.2.cloned.1.call-start = ((), (), s32[]{:S(2)}) async-start(), calls=%async_computation.4 | async-start | bytes 9830400 | tf_op jit(solution)/shard_map/all_gather | solution.py:81
  101.7 5.4 %copy-start.2 = (bf16[640,1536]{1,0:T(8,128)(2,1)S(1)}, bf16[640,1536]{1,0:T(8,128)(2,1)}, u32[]{:S(2)}) copy-start(bf16[640,1536]{1,0:T(8,128)(2,1)} %reshape.95) | copy-start | bytes 5898244
  105.7 72.8 %collective-permute-start = (bf16[640,1536]{1,0:T(8,128)(2,1)}, bf16[640,1536]{1,0:T(8,128)(2,1)}, u32[]{:S(2)}, u32[]{:S(2)}) collective-permute-start(bf16[640,1536]{1,0:T(8,128)(2,1)} %reshape.93), channel_id=1, source_target_pairs={{0,1},{1,2},{2,3},{3,0},{4,5},{5,6},{6,7},{7,4},{8,9},{9,10},{10,1... | collective-permute-start | bytes 5898248 | tf_op jit(solution)/shard_map/ppermute | solution.py:91
  107.0 11.9 %slice-start = ((s8[4718592]{0:T(1024)(128)(4,1)}), s8[4194304]{0:T(1024)(128)(4,1)S(1)}, s32[]{:S(2)}) async-start(s8[4718592]{0:T(1024)(128)(4,1)} %bitcast.61), calls=%async_computation.5 | async-start | bytes 8388608
  112.3 6.6 %copy-start.10 = (f32[640,1536]{1,0:T(8,128)}, f32[640,1536]{1,0:T(8,128)S(1)}, u32[]{:S(2)}) copy-start(f32[640,1536]{1,0:T(8,128)S(1)} %fusion.6) | copy-start | bytes 11796484
  112.4 6.6 %copy-start.3 = (bf16[640,1536]{1,0:T(8,128)(2,1)S(1)}, bf16[640,1536]{1,0:T(8,128)(2,1)}, u32[]{:S(2)}) copy-start(bf16[640,1536]{1,0:T(8,128)(2,1)} %reshape.93) | copy-start | bytes 5898244
  112.4 6.6 %slice-start.1 = ((s8[4718592]{0:T(1024)(128)(4,1)}), s8[524288]{0:T(1024)(128)(4,1)S(1)}, s32[]{:S(2)}) async-start(s8[4718592]{0:T(1024)(128)(4,1)} %bitcast.61), calls=%async_computation.6 | async-start | bytes 1048576
  119.0 5.4 %copy-start.8 = (f32[640,1536]{1,0:T(8,128)}, f32[640,1536]{1,0:T(8,128)S(1)}, u32[]{:S(2)}) copy-start(f32[640,1536]{1,0:T(8,128)S(1)} %fusion.2) | copy-start | bytes 11796484
  125.1 21.0 %all-to-all-start.3 = ((bf16[32,1,20]{2,1,0:T(2,128)(2,1)}), bf16[32,1,20]{2,1,0:T(2,128)(2,1)S(1)}, u32[]{:S(2)}, u32[]{:S(2)}) async-start(bf16[32,1,20]{2,1,0:T(2,128)(2,1)} %convert_element_type.97), calls=%async_computation.3 | async-start | bytes 32768 | tf_op jit(solution)/shard_map/all_to_all | solution.py:78
  129.1 9.0 %copy-start.9 = (f32[640,1536]{1,0:T(8,128)S(1)}, f32[640,1536]{1,0:T(8,128)}, u32[]{:S(2)}) copy-start(f32[640,1536]{1,0:T(8,128)} %copy-done.8) | copy-start | bytes 11796484
  129.2 9.0 %copy-start.11 = (f32[640,1536]{1,0:T(8,128)S(1)}, f32[640,1536]{1,0:T(8,128)}, u32[]{:S(2)}) copy-start(f32[640,1536]{1,0:T(8,128)} %get-tuple-element.12) | copy-start | bytes 11796484
  146.1 38.9 %all-to-all-start.2 = ((bf16[32,20,1536]{2,1,0:T(8,128)(2,1)}), bf16[32,20,1536]{2,1,0:T(8,128)(2,1)S(1)}, u32[]{:S(2)}, u32[]{:S(2)}) async-start(bf16[32,20,1536]{2,1,0:T(8,128)(2,1)} %reshape.96), calls=%async_computation.2 | async-start | bytes 4718592 | tf_op jit(solution)/shard_map/all_to_all | solution.py:78
  153.5 44.5 %collective-permute-start.1 = (bf16[640,1536]{1,0:T(8,128)(2,1)}, bf16[640,1536]{1,0:T(8,128)(2,1)}, u32[]{:S(2)}, u32[]{:S(2)}) collective-permute-start(bf16[640,1536]{1,0:T(8,128)(2,1)} %reshape.93), channel_id=1, source_target_pairs={{0,3},{1,0},{2,1},{3,2},{4,7},{5,4},{6,5},{7,6},{8,11},{9,8},{10,9... | collective-permute-start | bytes 5898248 | tf_op jit(solution)/shard_map/ppermute | solution.py:96
  178.6 45.4 %collective-permute-start.2 = (bf16[640,1536]{1,0:T(8,128)(2,1)}, bf16[640,1536]{1,0:T(8,128)(2,1)}, u32[]{:S(2)}, u32[]{:S(2)}) collective-permute-start(bf16[640,1536]{1,0:T(8,128)(2,1)} %collective-permute-done), channel_id=1, source_target_pairs={{0,1},{1,2},{2,3},{3,0},{4,5},{5,6},{6,7},{7,4},{8,9},{9,10},{10,1... | collective-permute-start | bytes 5898248 | tf_op jit(solution)/shard_map/ppermute | solution.py:91
  178.6 3.6 %copy-start.4 = (bf16[640,1536]{1,0:T(8,128)(2,1)S(1)}, bf16[640,1536]{1,0:T(8,128)(2,1)}, u32[]{:S(2)}) copy-start(bf16[640,1536]{1,0:T(8,128)(2,1)} %reshape.93) | copy-start | bytes 5898244
  182.2 1.7 copy-start.5
  236.8 7.8 %copy-start.6 = (bf16[2560,1536]{1,0:T(8,128)(2,1)S(1)}, bf16[2560,1536]{1,0:T(8,128)(2,1)}, u32[]{:S(2)}) copy-start(bf16[2560,1536]{1,0:T(8,128)(2,1)} %all-gather.2.cloned.1.call-done) | copy-start | bytes 23592964
  250.1 7.9 %copy-start.7 = (f32[2560,384]{1,0:T(8,128)S(1)}, f32[2560,384]{1,0:T(8,128)}, u32[]{:S(2)}) copy-start(f32[2560,384]{1,0:T(8,128)} %fusion.28) | copy-start | bytes 11796484
  262.6 4.4 %copy-start.1 = (bf16[128,1536]{1,0:T(8,128)(2,1)S(1)}, bf16[128,1536]{1,0:T(8,128)(2,1)}, u32[]{:S(2)}) copy-start(bf16[128,1536]{1,0:T(8,128)(2,1)} %param.10) | copy-start | bytes 1179652
Sparse Core Ops, SparseCore 0:
  59.5 102.8 all-gather.1
